TPU v7x, 32 devices: a whole 2x2x4 slice. The times are simulated.
32 devices in a mesh: col: 8 (over z, y), row: 4 (over x, core).
Axes of the slice: x: 2, y: 2, z: 4, core: 2. Of those that a mesh axis runs over, the one named last changes fastest.
Arguments:
- right_side: float32 [8192, 256], P(('row', 'col')), may hold values from -6 to 6
- prior_solution: bfloat16 [16384, 256], P('col'), may hold values from -6 to 6
- factor_codes: bfloat16 [8192, 16384], P('row', 'col'), may hold values from -0.046875 to 0.046875
- block_scale: float32 [4, 64], P('row', 'col'), may hold values from 0.3 to 3
- diag_inverse: bfloat16 [4, 2048, 2048], P('row', 'col'), may hold values from -0.125 to 0.125
- inner_factor: bfloat16 [4, 4, 2048, 2048], P('row', None, 'col'), may hold values from -0.125 to 0.125
Outputs:
- solved: float32 [8192, 256], P(('row', 'col'))
All inputs are finite; a program needn't handle non-finite values.
Results may differ from a plain program's by a relative error of at most 0.0095.
Values may be sent and summed in bfloat16 or wider, within the bound.
No kernel may reach another device: no remote copies, remote signals or barrier semaphores. Data moves between devices by JAX's collectives and lax.ppermute only.
A program may use at most 64 MiB of HBM per device.

v0:
```python
import jax
import jax.numpy as jnp
from jax import lax
from jax.sharding import PartitionSpec as P


def from_root(value, axis, source):
    kept = jnp.where(lax.axis_index(axis) == source, value, 0).astype(value.dtype)
    return lax.psum(kept, axis)


def local(right_side, prior_solution, factor_codes, block_scale, diag_inverse, inner_factor):
    rows_each = right_side.shape[0]
    panel_rows = factor_codes.shape[0]
    blocks_here = block_scale.shape[1]
    block_cols = factor_codes.shape[1] // blocks_here
    columns_out = right_side.shape[1]
    summed = jnp.zeros((panel_rows, columns_out), jnp.float32)
    for column_block in range(blocks_here):
        coded = lax.dynamic_slice(
            factor_codes, (0, column_block * block_cols), (panel_rows, block_cols)
        )
        earlier = prior_solution[column_block * block_cols : (column_block + 1) * block_cols]
        summed = summed + block_scale[0, column_block] * jnp.dot(
            coded, earlier, preferred_element_type=jnp.float32
        )
    prior_rows = lax.psum_scatter(summed, "col", scatter_dimension=0, tiled=True)
    rhs = right_side - prior_rows
    row_place = lax.axis_index("row")
    solved = jnp.zeros((rows_each, columns_out), jnp.float32)
    inverse_rows = diag_inverse[0]
    panel_count = lax.axis_size("row")
    for section in range(panel_count):
        rounded = rhs.astype(jnp.bfloat16)
        current = jnp.dot(
            inverse_rows,
            lax.all_gather(rounded, "col", axis=0, tiled=True),
            preferred_element_type=jnp.float32,
        )
        solved = jnp.where(row_place == section, current, solved)
        if section + 1 < panel_count:
            sending = current.astype(jnp.bfloat16)
            coupling = inner_factor[0, section]
            whole_panel = lax.all_gather(sending, "col", axis=0, tiled=True)
            copied = from_root(whole_panel, "row", section)
            update = jnp.dot(coupling, copied, preferred_element_type=jnp.float32)
            rhs = rhs - jnp.where(row_place > section, update, 0.0)
    return solved


def solution(mesh):
    return jax.shard_map(
        local,
        mesh=mesh,
        in_specs=(
            P(("row", "col"), None),
            P("col", None),
            P("row", "col"),
            P("row", "col"),
            P("row", "col", None),
            P("row", None, "col", None),
        ),
        out_specs=P(("row", "col"), None),
        check_vma=False,
    )
```

profile of v0, /device:TPU:0, one launch (start us, length us, event | category | flops | bytes accessed | tf_op | source)
XLA Modules:
  0.0 509.4 jit_solution(15707440207164434849)
XLA Ops:
  6.5 1.6 fusion.45
  8.2 2.5 convolution_multiply_fusion.7
  10.7 2.5 fusion.6
  13.3 2.0 fusion.5
  15.3 1.1 fusion.4
  16.4 1.1 fusion.3
  17.5 1.1 fusion.2
  18.6 1.0 fusion.1
  19.6 2.4 fusion
  22.1 71.2 %reduce-scatter.2.cloned.1.call-done = f32[256,256]{1,0:T(8,128)} async-done(((f32[2048,256]{1,0:T(8,128)}), f32[256,256]{1,0:T(8,128)}) %reduce-scatter.2.cloned.1.call-update) | async-done | bytes 262160 | tf_op jit(solution)/shard_map/reduce_scatter | solution.py:27
  93.2 1.6 fusion.44
  95.0 39.7 %all-gather.8.cloned.1.call-done = bf16[2048,256]{1,0:T(8,128)(2,1)} async-done(((bf16[256,256]{1,0:T(8,128)(2,1)}), bf16[2048,256]{1,0:T(8,128)(2,1)}) %all-gather.8.cloned.1.call-update) | async-done | bytes 1048592 | tf_op jit(solution)/shard_map/all_gather | solution.py:37
  134.7 1.7 fusion.23
  136.4 0.7 convert_bitcast_fusion.2
  137.2 38.2 %all-gather.10.cloned.1.call-done = bf16[2048,256]{0,1:T(8,128)(2,1)} async-done(((bf16[256,256]{0,1:T(8,128)(2,1)}), bf16[2048,256]{0,1:T(8,128)(2,1)}) %all-gather.10.cloned.1.call-update) | async-done | bytes 1048592 | tf_op jit(solution)/shard_map/all_gather | solution.py:44
  175.4 2.3 broadcast_select_fusion.2
  177.7 35.2 %all-reduce.4.cloned.1.call-done = bf16[2048,256]{0,1:T(8,128)(2,1)} async-done(((bf16[2048,256]{0,1:T(8,128)(2,1)}), bf16[2048,256]{0,1:T(8,128)(2,1)}) %all-reduce.4.cloned.1.call-update) | async-done | bytes 1048592 | tf_op jit(solution)/shard_map/psum | solution.py:9
  212.9 2.7 fusion.46
  215.7 40.9 %all-gather.12.cloned.1.call-done = bf16[2048,256]{1,0:T(8,128)(2,1)} async-done(((bf16[256,256]{1,0:T(8,128)(2,1)}), bf16[2048,256]{1,0:T(8,128)(2,1)}) %all-gather.12.cloned.1.call-update) | async-done | bytes 1048592 | tf_op jit(solution)/shard_map/all_gather | solution.py:37
  256.5 1.7 fusion.21
  259.0 38.2 %all-gather.14.cloned.1.call-done = bf16[2048,256]{0,1:T(8,128)(2,1)} async-done(((bf16[256,256]{0,1:T(8,128)(2,1)}), bf16[2048,256]{0,1:T(8,128)(2,1)}) %all-gather.14.cloned.1.call-update) | async-done | bytes 1048592 | tf_op jit(solution)/shard_map/all_gather | solution.py:44
  297.2 1.1 broadcast_select_fusion.1
  298.3 36.5 %all-reduce.6.cloned.1.call-done = bf16[2048,256]{0,1:T(8,128)(2,1)} async-done(((bf16[2048,256]{0,1:T(8,128)(2,1)}), bf16[2048,256]{0,1:T(8,128)(2,1)}) %all-reduce.6.cloned.1.call-update) | async-done | bytes 1048592 | tf_op jit(solution)/shard_map/psum | solution.py:9
  334.9 2.7 fusion.47
  337.6 40.9 %all-gather.16.cloned.1.call-done = bf16[2048,256]{1,0:T(8,128)(2,1)} async-done(((bf16[256,256]{1,0:T(8,128)(2,1)}), bf16[2048,256]{1,0:T(8,128)(2,1)}) %all-gather.16.cloned.1.call-update) | async-done | bytes 1048592 | tf_op jit(solution)/shard_map/all_gather | solution.py:37
  378.5 1.7 fusion.19
  381.0 38.2 %all-gather.18.cloned.1.call-done = bf16[2048,256]{0,1:T(8,128)(2,1)} async-done(((bf16[256,256]{0,1:T(8,128)(2,1)}), bf16[2048,256]{0,1:T(8,128)(2,1)}) %all-gather.18.cloned.1.call-update) | async-done | bytes 1048592 | tf_op jit(solution)/shard_map/all_gather | solution.py:44
  419.2 1.1 broadcast_select_fusion
  420.3 36.6 %all-reduce.8.cloned.1.call-done = bf16[2048,256]{0,1:T(8,128)(2,1)} async-done(((bf16[2048,256]{0,1:T(8,128)(2,1)}), bf16[2048,256]{0,1:T(8,128)(2,1)}) %all-reduce.8.cloned.1.call-update) | async-done | bytes 1048592 | tf_op jit(solution)/shard_map/psum | solution.py:9
  456.9 2.7 fusion.14
  460.0 40.5 %all-gather.20.cloned.1.call-done = bf16[2048,256]{1,0:T(8,128)(2,1)} async-done(((bf16[256,256]{1,0:T(8,128)(2,1)}), bf16[2048,256]{1,0:T(8,128)(2,1)}) %all-gather.20.cloned.1.call-update) | async-done | bytes 1048592 | tf_op jit(solution)/shard_map/all_gather | solution.py:37
  500.5 2.4 fusion.7
  (35 shorter events, 2.3 us)
Async XLA Ops:
  6.5 128.2 %copy-start = (bf16[1,256,2048]{2,1,0:T(8,128)(2,1)S(1)}, bf16[1,256,2048]{2,1,0:T(8,128)(2,1)}, u32[]{:S(2)}) copy-start(bf16[1,256,2048]{2,1,0:T(8,128)(2,1)} %param.10) | copy-start | bytes 3145732
  6.5 86.7 %reduce-scatter.2.cloned.1.call-start = ((), (), s32[]{:S(2)}) async-start(), calls=%async_computation.1 | async-start | bytes 2359296 | tf_op jit(solution)/shard_map/reduce_scatter | solution.py:27
  8.2 5.1 copy-start.1
  13.3 2.0 copy-start.2
  22.0 71.2 %copy-start.3 = (f32[256,256]{1,0:T(8,128)S(1)}, f32[256,256]{1,0:T(8,128)}, u32[]{:S(2)}) copy-start(f32[256,256]{1,0:T(8,128)} %param.6) | copy-start | bytes 786436
  22.0 112.7 %all-gather.8.cloned.1.call-start = ((), (), s32[]{:S(2)}) async-start(), calls=%async_computation.2 | async-start | bytes 1179648 | tf_op jit(solution)/shard_map/all_gather | solution.py:37
  94.9 80.5 %all-gather.10.cloned.1.call-start = ((), (), s32[]{:S(2)}) async-start(), calls=%async_computation.3 | async-start | bytes 1179648 | tf_op jit(solution)/shard_map/all_gather | solution.py:44
  137.1 75.8 %all-reduce.4.cloned.1.call-start = ((), (), s32[]{:S(2)}) async-start(), calls=%async_computation.4 | async-start | bytes 2097152 | tf_op jit(solution)/shard_map/psum | solution.py:9
  177.7 78.9 %all-gather.12.cloned.1.call-start = ((), (), s32[]{:S(2)}) async-start(), calls=%async_computation.5 | async-start | bytes 1179648 | tf_op jit(solution)/shard_map/all_gather | solution.py:37
  215.6 81.6 %all-gather.14.cloned.1.call-start = ((), (), s32[]{:S(2)}) async-start(), calls=%async_computation.6 | async-start | bytes 1179648 | tf_op jit(solution)/shard_map/all_gather | solution.py:44
  258.9 75.9 %all-reduce.6.cloned.1.call-start = ((), (), s32[]{:S(2)}) async-start(), calls=%async_computation.7 | async-start | bytes 2097152 | tf_op jit(solution)/shard_map/psum | solution.py:9
  298.3 80.2 %all-gather.16.cloned.1.call-start = ((), (), s32[]{:S(2)}) async-start(), calls=%async_computation.8 | async-start | bytes 1179648 | tf_op jit(solution)/shard_map/all_gather | solution.py:37
  337.6 81.6 %all-gather.18.cloned.1.call-start = ((), (), s32[]{:S(2)}) async-start(), calls=%async_computation.9 | async-start | bytes 1179648 | tf_op jit(solution)/shard_map/all_gather | solution.py:44
  380.9 76.0 %all-reduce.8.cloned.1.call-start = ((), (), s32[]{:S(2)}) async-start(), calls=%async_computation.10 | async-start | bytes 2097152 | tf_op jit(solution)/shard_map/psum | solution.py:9
  420.2 80.3 %all-gather.20.cloned.1.call-start = ((), (), s32[]{:S(2)}) async-start(), calls=%async_computation.11 | async-start | bytes 1179648 | tf_op jit(solution)/shard_map/all_gather | solution.py:37
Sparse Core Ops, SparseCore 0:
  22.2 71.0 reduce-scatter.1
  95.4 39.2 all-gather.7
  137.2 38.0 all-gather.9
  177.8 35.0 all-reduce.3
  215.8 40.7 all-gather.11
  259.1 38.0 all-gather.13
  299.6 35.2 all-reduce.5
  337.7 40.7 all-gather.15
  381.0 38.0 all-gather.17
  421.4 35.4 all-reduce.7
  459.7 40.7 all-gather.19
where the time goes:
time: 510 us; the launch traced here: 509 us
  waiting for transfers between devices  456 us (89%)
  matrix products  29.3 us (6%)
  between operations  13.4 us (3%)
  other arithmetic  8.06 us (2%)
    all_gather x4, waiting for transfers between devices, local(): lax.all_gather(rounded, 'col', axis=0, tiled=True)  162 us
    all_gather x3, waiting for transfers between devices, local(): whole_panel = lax.all_gather(sending, 'col', axis=0, tiled=True)  115 us
    psum x3, waiting for transfers between devices, from_root(): return lax.psum(kept, axis)  108 us
    reduce_scatter x1, waiting for transfers between devices, local(): lax.psum_scatter(summed, 'col', scatter_dimension=0, tiled=True)  71.2 us
    dot_general x8, matrix products, local(): jnp.dot(coded, earlier, preferred_element_type=jnp.float32)  13.7 us
  transfers between devices with their start and end apart: 11, of which 11 were waited for; matrix products, arithmetic and copies ran while one was open for 0% of the time, Pallas kernels for 0%

commit v1 on v0

--- a/solution.py
+++ b/solution.py
@@ -6,7 +6,7 @@
 
 def from_root(value, axis, source):
     kept = jnp.where(lax.axis_index(axis) == source, value, 0).astype(value.dtype)
-    return lax.psum(kept, axis)
+    return jnp.sum(lax.all_gather(kept, axis), axis=0)
 
 
 def local(right_side, prior_solution, factor_codes, block_scale, diag_inverse, inner_factor):

time: 510 us -> 547 us (1.073)
  local copies, waits for them, and re-layouts: 2.03 us -> 25.7 us
  other arithmetic: 8.06 us -> 30.2 us
  waiting for transfers between devices: 456 us -> 447 us
    psum x3 -> x0, waiting for transfers between devices: 108 us -> none  [from_root(): return lax.psum(kept, axis)]
    all_gather x0 -> x3, waiting for transfers between devices: none -> 101 us  [from_root(): return jnp.sum(lax.all_gather(kept, axis), axis=0)]
    all_gather x0 -> x3, local copies, waits for them, and re-layouts: none -> 23.7 us  [from_root(): return jnp.sum(lax.all_gather(kept, axis), axis=0)]
    reduce_sum x0 -> x3, other arithmetic: none -> 22 us  [from_root(): return jnp.sum(lax.all_gather(kept, axis), axis=0)]
where the time goes in v1:
time: 547 us; the launch traced here: 546 us
  waiting for transfers between devices  447 us (82%)
  other arithmetic  30.2 us (6%)
  matrix products  28.3 us (5%)
  local copies, waits for them, and re-layouts  25.7 us (5%)
  between operations  13.4 us (2%)
    all_gather x4, waiting for transfers between devices, local(): lax.all_gather(rounded, 'col', axis=0, tiled=True)  161 us
    all_gather x3, waiting for transfers between devices, local(): whole_panel = lax.all_gather(sending, 'col', axis=0, tiled=True)  115 us
    all_gather x3, waiting for transfers between devices, from_root(): return jnp.sum(lax.all_gather(kept, axis), axis=0)  101 us
    reduce_scatter x1, waiting for transfers between devices, local(): lax.psum_scatter(summed, 'col', scatter_dimension=0, tiled=True)  71.2 us
    all_gather x3, local copies, waits for them, and re-layouts, from_root(): return jnp.sum(lax.all_gather(kept, axis), axis=0)  23.7 us
    reduce_sum x3, other arithmetic, from_root(): return jnp.sum(lax.all_gather(kept, axis), axis=0)  22 us
    dot_general x8, matrix products, local(): jnp.dot(coded, earlier, preferred_element_type=jnp.float32)  13.7 us
  transfers between devices with their start and end apart: 11, of which 11 were waited for; matrix products, arithmetic and copies ran while one was open for 0% of the time, Pallas kernels for 0%

profile of v1, /device:TPU:0, one launch (start us, length us, event | category | flops | bytes accessed | tf_op | source)
XLA Modules:
  0.0 545.9 jit_solution(1188398663806459015)
XLA Ops:
  6.5 1.6 fusion.45
  8.2 2.5 convolution_multiply_fusion.7
  10.7 2.5 fusion.6
  13.3 2.0 fusion.5
  15.3 1.1 fusion.4
  19.6 2.4 fusion
  22.1 71.2 %reduce-scatter.2.cloned.1.call-done = f32[256,256]{1,0:T(8,128)} async-done(((f32[2048,256]{1,0:T(8,128)}), f32[256,256]{1,0:T(8,128)}) %reduce-scatter.2.cloned.1.call-update) | async-done | bytes 262160 | tf_op jit(solution)/shard_map/reduce_scatter | solution.py:27
  93.3 1.6 fusion.44
  95.0 39.7 %all-gather.14.cloned.1.call-done = bf16[2048,256]{1,0:T(8,128)(2,1)} async-done(((bf16[256,256]{1,0:T(8,128)(2,1)}), bf16[2048,256]{1,0:T(8,128)(2,1)}) %all-gather.14.cloned.1.call-update) | async-done | bytes 1048592 | tf_op jit(solution)/shard_map/all_gather | solution.py:37
  134.7 1.7 fusion.23
  137.2 38.2 %all-gather.16.cloned.1.call-done = bf16[2048,256]{0,1:T(8,128)(2,1)} async-done(((bf16[256,256]{0,1:T(8,128)(2,1)}), bf16[2048,256]{0,1:T(8,128)(2,1)}) %all-gather.16.cloned.1.call-update) | async-done | bytes 1048592 | tf_op jit(solution)/shard_map/all_gather | solution.py:44
  175.4 2.3 broadcast_select_fusion.2
  177.8 32.7 %all-gather.28.cloned.1.call-done = bf16[8192,256]{0,1:T(8,128)(2,1)} async-done(((bf16[2048,256]{0,1:T(8,128)(2,1)}), bf16[8192,256]{0,1:T(8,128)(2,1)}) %all-gather.28.cloned.1.call-update) | async-done | bytes 4194320 | tf_op jit(solution)/shard_map/all_gather | solution.py:9
  210.5 7.9 %reshape = bf16[4,2048,256]{1,0,2:T(4,128)(2,1)} reshape(bf16[8192,256]{0,1:T(8,128)(2,1)} %all-gather.28.cloned.1.call-done) | data formatting | bytes 8388608 | tf_op jit(solution)/shard_map/all_gather | solution.py:9
  218.4 7.3 %reduce_sum.36 = bf16[2048,256]{0,1:T(8,128)(2,1)S(1)} reduce(bf16[4,2048,256]{1,0,2:T(4,128)(2,1)} %reshape, bf16[]{:T(256)} %constant.16.clone.1), dimensions={0}, to_apply=%region_1.2 | reduce | flops 1572864 | bytes 5242882 | tf_op jit(solution)/shard_map/reduce_sum | solution.py:9
  225.7 2.4 fusion.46
  228.1 40.4 %all-gather.18.cloned.1.call-done = bf16[2048,256]{1,0:T(8,128)(2,1)} async-done(((bf16[256,256]{1,0:T(8,128)(2,1)}), bf16[2048,256]{1,0:T(8,128)(2,1)}) %all-gather.18.cloned.1.call-update) | async-done | bytes 1048592 | tf_op jit(solution)/shard_map/all_gather | solution.py:37
  268.5 1.7 fusion.21
  271.0 38.2 %all-gather.20.cloned.1.call-done = bf16[2048,256]{0,1:T(8,128)(2,1)} async-done(((bf16[256,256]{0,1:T(8,128)(2,1)}), bf16[2048,256]{0,1:T(8,128)(2,1)}) %all-gather.20.cloned.1.call-update) | async-done | bytes 1048592 | tf_op jit(solution)/shard_map/all_gather | solution.py:44
  310.5 33.7 %all-gather.30.cloned.1.call-done = bf16[8192,256]{0,1:T(8,128)(2,1)} async-done(((bf16[2048,256]{0,1:T(8,128)(2,1)}), bf16[8192,256]{0,1:T(8,128)(2,1)}) %all-gather.30.cloned.1.call-update) | async-done | bytes 4194320 | tf_op jit(solution)/shard_map/all_gather | solution.py:9
  344.3 7.9 %reshape.1 = bf16[4,2048,256]{1,0,2:T(4,128)(2,1)} reshape(bf16[8192,256]{0,1:T(8,128)(2,1)} %all-gather.30.cloned.1.call-done) | data formatting | bytes 8388608 | tf_op jit(solution)/shard_map/all_gather | solution.py:9
  352.2 7.3 %reduce_sum.37 = bf16[2048,256]{0,1:T(8,128)(2,1)S(1)} reduce(bf16[4,2048,256]{1,0,2:T(4,128)(2,1)} %reshape.1, bf16[]{:T(256)} %constant.16.clone.1), dimensions={0}, to_apply=%region_2.3 | reduce | flops 1572864 | bytes 5242882 | tf_op jit(solution)/shard_map/reduce_sum | solution.py:9
  359.5 2.4 fusion.47
  362.0 40.4 %all-gather.22.cloned.1.call-done = bf16[2048,256]{1,0:T(8,128)(2,1)} async-done(((bf16[256,256]{1,0:T(8,128)(2,1)}), bf16[2048,256]{1,0:T(8,128)(2,1)}) %all-gather.22.cloned.1.call-update) | async-done | bytes 1048592 | tf_op jit(solution)/shard_map/all_gather | solution.py:37
  402.3 1.7 fusion.19
  404.8 38.2 %all-gather.24.cloned.1.call-done = bf16[2048,256]{0,1:T(8,128)(2,1)} async-done(((bf16[256,256]{0,1:T(8,128)(2,1)}), bf16[2048,256]{0,1:T(8,128)(2,1)}) %all-gather.24.cloned.1.call-update) | async-done | bytes 1048592 | tf_op jit(solution)/shard_map/all_gather | solution.py:44
  444.4 34.6 %all-gather.32.cloned.1.call-done = bf16[8192,256]{0,1:T(8,128)(2,1)} async-done(((bf16[2048,256]{0,1:T(8,128)(2,1)}), bf16[8192,256]{0,1:T(8,128)(2,1)}) %all-gather.32.cloned.1.call-update) | async-done | bytes 4194320 | tf_op jit(solution)/shard_map/all_gather | solution.py:9
  479.0 7.9 %reshape.2 = bf16[4,2048,256]{1,0,2:T(4,128)(2,1)} reshape(bf16[8192,256]{0,1:T(8,128)(2,1)} %all-gather.32.cloned.1.call-done) | data formatting | bytes 8388608 | tf_op jit(solution)/shard_map/all_gather | solution.py:9
  486.9 7.3 %reduce_sum.38 = bf16[2048,256]{0,1:T(8,128)(2,1)S(1)} reduce(bf16[4,2048,256]{1,0,2:T(4,128)(2,1)} %reshape.2, bf16[]{:T(256)} %constant.16.clone.1), dimensions={0}, to_apply=%region_3.4 | reduce | flops 1572864 | bytes 5242882 | tf_op jit(solution)/shard_map/reduce_sum | solution.py:9
  494.2 2.4 fusion.14
  497.0 40.0 %all-gather.26.cloned.1.call-done = bf16[2048,256]{1,0:T(8,128)(2,1)} async-done(((bf16[256,256]{1,0:T(8,128)(2,1)}), bf16[2048,256]{1,0:T(8,128)(2,1)}) %all-gather.26.cloned.1.call-update) | async-done | bytes 1048592 | tf_op jit(solution)/shard_map/all_gather | solution.py:37
  537.0 2.4 fusion.7
  (41 shorter events, 8.7 us)
Async XLA Ops:
  6.5 128.2 %copy-start = (bf16[1,256,2048]{2,1,0:T(8,128)(2,1)S(1)}, bf16[1,256,2048]{2,1,0:T(8,128)(2,1)}, u32[]{:S(2)}) copy-start(bf16[1,256,2048]{2,1,0:T(8,128)(2,1)} %param.10) | copy-start | bytes 3145732
  6.5 86.8 %reduce-scatter.2.cloned.1.call-start = ((), (), s32[]{:S(2)}) async-start(), calls=%async_computation.1 | async-start | bytes 2359296 | tf_op jit(solution)/shard_map/reduce_scatter | solution.py:27
  8.2 5.1 copy-start.1
  13.3 2.0 copy-start.2
  22.0 71.3 %copy-start.3 = (f32[256,256]{1,0:T(8,128)S(1)}, f32[256,256]{1,0:T(8,128)}, u32[]{:S(2)}) copy-start(f32[256,256]{1,0:T(8,128)} %param.6) | copy-start | bytes 786436
  22.0 112.7 %all-gather.14.cloned.1.call-start = ((), (), s32[]{:S(2)}) async-start(), calls=%async_computation.2 | async-start | bytes 1179648 | tf_op jit(solution)/shard_map/all_gather | solution.py:37
  95.0 80.5 %all-gather.16.cloned.1.call-start = ((), (), s32[]{:S(2)}) async-start(), calls=%async_computation.3 | async-start | bytes 1179648 | tf_op jit(solution)/shard_map/all_gather | solution.py:44
  137.1 73.3 %all-gather.28.cloned.1.call-start = ((), (), s32[]{:S(2)}) async-start(), calls=%async_computation.9 | async-start | bytes 5242880 | tf_op jit(solution)/shard_map/all_gather | solution.py:9
  177.7 90.8 %all-gather.18.cloned.1.call-start = ((), (), s32[]{:S(2)}) async-start(), calls=%async_computation.4 | async-start | bytes 1179648 | tf_op jit(solution)/shard_map/all_gather | solution.py:37
  228.1 81.1 %all-gather.20.cloned.1.call-start = ((), (), s32[]{:S(2)}) async-start(), calls=%async_computation.5 | async-start | bytes 1179648 | tf_op jit(solution)/shard_map/all_gather | solution.py:44
  270.9 73.3 %all-gather.30.cloned.1.call-start = ((), (), s32[]{:S(2)}) async-start(), calls=%async_computation.10 | async-start | bytes 5242880 | tf_op jit(solution)/shard_map/all_gather | solution.py:9
  310.3 92.0 %all-gather.22.cloned.1.call-start = ((), (), s32[]{:S(2)}) async-start(), calls=%async_computation.6 | async-start | bytes 1179648 | tf_op jit(solution)/shard_map/all_gather | solution.py:37
  361.9 81.1 %all-gather.24.cloned.1.call-start = ((), (), s32[]{:S(2)}) async-start(), calls=%async_computation.7 | async-start | bytes 1179648 | tf_op jit(solution)/shard_map/all_gather | solution.py:44
  404.7 74.2 %all-gather.32.cloned.1.call-start = ((), (), s32[]{:S(2)}) async-start(), calls=%async_computation.11 | async-start | bytes 5242880 | tf_op jit(solution)/shard_map/all_gather | solution.py:9
  444.1 92.9 %all-gather.26.cloned.1.call-start = ((), (), s32[]{:S(2)}) async-start(), calls=%async_computation.8 | async-start | bytes 1179648 | tf_op jit(solution)/shard_map/all_gather | solution.py:37
Sparse Core Ops, SparseCore 0:
  22.2 71.0 reduce-scatter.1
  95.4 39.2 all-gather.13
  137.3 38.0 all-gather.15
  177.9 32.5 all-gather.27
  228.2 40.2 all-gather.17
  271.1 38.0 all-gather.19
  310.8 33.4 all-gather.29
  362.0 40.2 all-gather.21
  404.9 38.0 all-gather.23
  444.4 34.4 all-gather.31
  496.7 40.2 all-gather.25
